TPU v7x, 32 devices: a whole 2x2x4 slice. The times are simulated.
32 devices in a mesh: dp: 8 (over z, y), group: 4 (over x, core).
Axes of the slice: x: 2, y: 2, z: 4, core: 2. Of those that a mesh axis runs over, the one named last changes fastest.
Arguments:
- tokens: bfloat16 [16384, 1024], P(('dp', 'group')), may hold values from -16 to 16
- segment_ids: int32 [16384], P(('dp', 'group')), may hold values from 0 to 3, as said below
- positions: int32 [16384], P(('dp', 'group')), may hold values from 0 to 1999, as said below
- cotangent: bfloat16 [16384, 1024], P(('dp', 'group')), may hold values from -6 to 6
- qkv_weight: float32 [1024, 4096], P('group'), may hold values from -1 to 1
- out_weight: float32 [2048, 1024], P('group'), may hold values from -1 to 1
- gate_up_weight: float32 [1024, 6144], P('group'), may hold values from -0.1875 to 0.1875
- down_weight: float32 [3072, 1024], P('group'), may hold values from -0.109375 to 0.109375
- norm_gains: float32 [2, 1024], P(None, 'group'), may hold values from 0.5 to 1.5
- head_gains: float32 [2, 128], P(None, 'group'), may hold values from 0.6 to 1.4
- qkv_moments: float32 [2, 1024, 4096], P(None, 'group'), as said below
- out_moments: float32 [2, 2048, 1024], P(None, 'group'), as said below
- gate_up_moments: float32 [2, 1024, 6144], P(None, 'group'), as said below
- down_moments: float32 [2, 3072, 1024], P(None, 'group'), as said below
- norm_moments: float32 [2, 2, 1024], P(None, None, 'group'), as said below
- head_moments: float32 [2, 2, 128], P(None, None, 'group'), as said below
Outputs:
- output: bfloat16 [16384, 1024], P(('dp', 'group'))
- tokens_grad: bfloat16 [16384, 1024], P(('dp', 'group'))
- qkv_grad: float32 [1024, 4096], P('group', 'dp')
- out_grad: float32 [2048, 1024], P('group', 'dp')
- gate_up_grad: float32 [1024, 6144], P('group', 'dp')
- down_grad: float32 [3072, 1024], P('group', 'dp')
- norm_grad: float32 [2, 1024], P(None, 'group')
- head_grad: float32 [2, 128], P(None, 'group')
- new_qkv_weight: float32 [1024, 4096], P('group')
- new_out_weight: float32 [2048, 1024], P('group')
- new_gate_up_weight: float32 [1024, 6144], P('group')
- new_down_weight: float32 [3072, 1024], P('group')
- new_norm_gains: float32 [2, 1024], P(None, 'group')
- new_head_gains: float32 [2, 128], P(None, 'group')
- new_qkv_moments: float32 [2, 1024, 4096], P(None, 'group')
- new_out_moments: float32 [2, 2048, 1024], P(None, 'group')
- new_gate_up_moments: float32 [2, 1024, 6144], P(None, 'group')
- new_down_moments: float32 [2, 3072, 1024], P(None, 'group')
- new_norm_moments: float32 [2, 2, 1024], P(None, None, 'group')
- new_head_moments: float32 [2, 2, 128], P(None, None, 'group')
Inputs may be any that keep to these rules, and one draw needn't show every extreme that they name: `segment_ids`: along each sequence of 512 consecutive tokens the ids never fall; equal ids within a sequence mark one document. A token's position counts from its document's first token, which may lie in an earlier sequence; within a document positions rise by one. `qkv_moments`: the second moments are positive. `out_moments`: the second moments are positive. `gate_up_moments`: the second moments are positive. `down_moments`: the second moments are positive. `norm_moments`: the second moments are positive. `head_moments`: the second moments are positive.
All inputs are finite; a program needn't handle non-finite values.
Results may differ from a plain program's by a relative error of at most 0.013.
The roundings to bfloat16 on the way count: a program that leaves them out, or rounds other values in their place, can miss the bound.
Values may be sent and summed in bfloat16 or wider, within the bound.
A program may use at most 320 MiB of HBM per device.

v0:
```python
import math
import jax
import jax.numpy as jnp
from jax import lax
from jax.sharding import PartitionSpec as P

HQ = 16
HK = 8
HD = 128
FF = 3072
SEQ_LEN = 512
PARAMS = 15730944
EPS_NORM = 1e-06
ROPE_BASE = 1000000.0
MASKED = -1e30
LEARN_RATE = 0.03
GAIN_RATE = 0.3
WEIGHT_DECAY = 0.1
BETA_ONE = 0.9
BETA_TWO = 0.95
ADAM_EPS = 1e-08
STEP_COUNT = 3.0


def rotary_tables(places, width):
    half_width = width // 2
    frequency = ROPE_BASE ** (-(jnp.arange(half_width, dtype=jnp.float32) * 2.0) / width)
    angles = places.astype(jnp.float32)[:, None] * frequency[None, :]
    return (jnp.cos(angles), jnp.sin(angles))


def rotate(values, cosine, sine_table):
    half_width = values.shape[-1] // 2
    front_half = values[..., :half_width]
    back_half = values[..., half_width:]
    cosine = cosine[:, None, :]
    sine_table = sine_table[:, None, :]
    return jnp.concatenate(
        [
            front_half * cosine - back_half * sine_table,
            back_half * cosine + front_half * sine_table,
        ],
        axis=-1,
    )


def contract_rows(left_side, right_side):
    return lax.dot_general(
        left_side, right_side, (((0,), (0,)), ((), ())), preferred_element_type=jnp.float32
    )


def contract_cols(left_side, right_side):
    return lax.dot_general(
        left_side, right_side, (((1,), (1,)), ((), ())), preferred_element_type=jnp.float32
    )


def norm_back(grad_out, normed, inv_root, gain):
    scaled = grad_out * gain
    return inv_root * (scaled - normed * jnp.mean(normed * scaled, axis=-1, keepdims=True))


def joined_order(gradient, along, owners, copies):
    layout = gradient.shape
    pieces_shape = (
        layout[:along] + (owners, copies, layout[along] // (owners * copies)) + layout[along + 1 :]
    )
    return jnp.swapaxes(gradient.reshape(pieces_shape), along, along + 1).reshape(layout)


def own_columns(gradient, index, count):
    width = gradient.shape[1] // count
    return lax.dynamic_slice_in_dim(gradient, index * width, width, 1)


def adam_update(master, moment, gradient, factor, step_rate, decay_rate):
    clipped = gradient * factor
    first_moment = BETA_ONE * moment[0] + (1.0 - BETA_ONE) * clipped
    second = BETA_TWO * moment[1] + (1.0 - BETA_TWO) * clipped * clipped
    first_hat = first_moment / (1.0 - BETA_ONE**STEP_COUNT)
    second_hat = second / (1.0 - BETA_TWO**STEP_COUNT)
    renewed = master - step_rate * (
        first_hat / (jnp.sqrt(second_hat) + ADAM_EPS) + decay_rate * master
    )
    return (renewed, jnp.stack([first_moment, second]))


def on_device(
    tokens,
    segment_ids,
    positions,
    cotangent,
    qkv_weight,
    out_weight,
    gate_up_weight,
    down_weight,
    norm_gains,
    head_gains,
    qkv_moments,
    out_moments,
    gate_up_moments,
    down_moments,
    norm_moments,
    head_moments,
):
    full_qkv, full_out, full_gate_up, full_down, full_norm, full_head = (
        lax.all_gather(qkv_weight.astype(jnp.bfloat16), "group", axis=0, tiled=True),
        lax.all_gather(out_weight.astype(jnp.bfloat16), "group", axis=0, tiled=True),
        lax.all_gather(gate_up_weight.astype(jnp.bfloat16), "group", axis=0, tiled=True),
        lax.all_gather(down_weight.astype(jnp.bfloat16), "group", axis=0, tiled=True),
        lax.all_gather(norm_gains.astype(jnp.bfloat16), "group", axis=1, tiled=True),
        lax.all_gather(head_gains.astype(jnp.bfloat16), "group", axis=1, tiled=True),
    )
    token_rows = tokens.shape[0]
    seq_count = token_rows // SEQ_LEN
    groups = HQ // HK
    inv_head = 1.0 / math.sqrt(HD)
    gain_one = full_norm[0].astype(jnp.float32)
    gain_two = full_norm[1].astype(jnp.float32)
    gain_query = full_head[0].astype(jnp.float32)
    gain_key = full_head[1].astype(jnp.float32)
    inputs = tokens.astype(jnp.float32)
    root_one = lax.rsqrt(jnp.mean(inputs * inputs, axis=-1, keepdims=True) + EPS_NORM)
    normed_one = inputs * root_one
    hidden_one = (normed_one * gain_one).astype(jnp.bfloat16)
    projected = jnp.dot(hidden_one, full_qkv, preferred_element_type=jnp.float32)
    query_raw = projected[:, : HQ * HD].reshape(token_rows, HQ, HD)
    key_raw = projected[:, HQ * HD : (HQ + HK) * HD].reshape(token_rows, HK, HD)
    value_low = projected[:, (HQ + HK) * HD :].reshape(token_rows, HK, HD).astype(jnp.bfloat16)
    cosine, sine_table = rotary_tables(positions, HD)
    query_root = lax.rsqrt(jnp.mean(query_raw * query_raw, axis=-1, keepdims=True) + EPS_NORM)
    query_normed = query_raw * query_root
    query_low = rotate(query_normed * gain_query, cosine, sine_table).astype(jnp.bfloat16)
    key_root = lax.rsqrt(jnp.mean(key_raw * key_raw, axis=-1, keepdims=True) + EPS_NORM)
    key_normed = key_raw * key_root
    key_low = rotate(key_normed * gain_key, cosine, sine_table).astype(jnp.bfloat16)
    query_blocks = query_low.reshape(seq_count, SEQ_LEN, HK, groups, HD)
    key_blocks = key_low.reshape(seq_count, SEQ_LEN, HK, HD)
    value_blocks = value_low.reshape(seq_count, SEQ_LEN, HK, HD)
    seg_blocks = segment_ids.reshape(seq_count, SEQ_LEN)
    places_idx = jnp.arange(SEQ_LEN)
    allowed = (seg_blocks[:, :, None] == seg_blocks[:, None, :]) & (
        places_idx[:, None] >= places_idx[None, :]
    )[None]
    allowed = allowed[:, None, None, :, :]

    def scores_of():
        raw_scores = (
            jnp.einsum(
                "sqkgd,spkd->skgqp", query_blocks, key_blocks, preferred_element_type=jnp.float32
            )
            * inv_head
        )
        return jnp.where(allowed, raw_scores, MASKED)

    scores = scores_of()
    row_peak = jnp.max(scores, axis=-1, keepdims=True)
    exp_total = jnp.sum(jnp.exp(scores - row_peak), axis=-1, keepdims=True)
    log_total = row_peak + jnp.log(exp_total)
    probs_low = jnp.exp(scores - log_total).astype(jnp.bfloat16)
    mixed_heads = jnp.einsum(
        "skgqp,spkd->sqkgd", probs_low, value_blocks, preferred_element_type=jnp.float32
    )
    mixed_low = mixed_heads.reshape(token_rows, HQ * HD).astype(jnp.bfloat16)
    attended = jnp.dot(mixed_low, full_out, preferred_element_type=jnp.float32)
    residual = inputs + attended
    root_two = lax.rsqrt(jnp.mean(residual * residual, axis=-1, keepdims=True) + EPS_NORM)
    normed_two = residual * root_two
    hidden_two = (normed_two * gain_two).astype(jnp.bfloat16)
    gate_up = jnp.dot(hidden_two, full_gate_up, preferred_element_type=jnp.float32)
    gate_part = gate_up[:, :FF]
    upward = gate_up[:, FF:]
    sigmoid_gate = jax.nn.sigmoid(gate_part)
    activated = (gate_part * sigmoid_gate * upward).astype(jnp.bfloat16)
    branch = jnp.dot(activated, full_down, preferred_element_type=jnp.float32)
    output = (residual + branch).astype(jnp.bfloat16)
    upstream = cotangent.astype(jnp.float32)
    down_local = contract_rows(activated, cotangent)
    grad_act = contract_cols(cotangent, full_down)
    grad_gate = grad_act * upward * sigmoid_gate * (1.0 + gate_part * (1.0 - sigmoid_gate))
    grad_up = grad_act * gate_part * sigmoid_gate
    grad_gate_up = jnp.concatenate([grad_gate, grad_up], axis=-1).astype(jnp.bfloat16)
    gate_up_local = contract_rows(hidden_two, grad_gate_up)
    grad_hidden_two = contract_cols(grad_gate_up, full_gate_up)
    grad_gain_two = jnp.sum(grad_hidden_two * normed_two, axis=0)
    grad_residual = upstream + norm_back(grad_hidden_two, normed_two, root_two, gain_two)
    residual_low = grad_residual.astype(jnp.bfloat16)
    out_local = contract_rows(mixed_low, residual_low)
    grad_mixed = (
        contract_cols(residual_low, full_out)
        .astype(jnp.bfloat16)
        .reshape(seq_count, SEQ_LEN, HK, groups, HD)
    )
    attn_probs = jnp.exp(scores_of() - log_total)
    grad_probs = jnp.einsum(
        "sqkgd,spkd->skgqp", grad_mixed, value_blocks, preferred_element_type=jnp.float32
    )
    grad_value = jnp.einsum(
        "skgqp,sqkgd->spkd",
        attn_probs.astype(jnp.bfloat16),
        grad_mixed,
        preferred_element_type=jnp.float32,
    )
    grad_scores = (
        attn_probs * (grad_probs - jnp.sum(attn_probs * grad_probs, axis=-1, keepdims=True))
    ).astype(jnp.bfloat16)
    grad_query = (
        jnp.einsum("skgqp,spkd->sqkgd", grad_scores, key_blocks, preferred_element_type=jnp.float32)
        * inv_head
    )
    grad_key = (
        jnp.einsum(
            "skgqp,sqkgd->spkd", grad_scores, query_blocks, preferred_element_type=jnp.float32
        )
        * inv_head
    )
    grad_query = rotate(grad_query.reshape(token_rows, HQ, HD), cosine, -sine_table)
    grad_key = rotate(grad_key.reshape(token_rows, HK, HD), cosine, -sine_table)
    grad_gain_query = jnp.sum(grad_query * query_normed, axis=(0, 1))
    grad_gain_key = jnp.sum(grad_key * key_normed, axis=(0, 1))
    grad_query_raw = norm_back(grad_query, query_normed, query_root, gain_query)
    grad_key_raw = norm_back(grad_key, key_normed, key_root, gain_key)
    grad_projected = jnp.concatenate(
        [
            grad_query_raw.reshape(token_rows, HQ * HD),
            grad_key_raw.reshape(token_rows, HK * HD),
            grad_value.reshape(token_rows, HK * HD),
        ],
        axis=-1,
    ).astype(jnp.bfloat16)
    qkv_local = contract_rows(hidden_one, grad_projected)
    grad_hidden_one = contract_cols(grad_projected, full_qkv)
    grad_gain_one = jnp.sum(grad_hidden_one * normed_one, axis=0)
    grad_inputs = grad_residual + norm_back(grad_hidden_one, normed_one, root_one, gain_one)
    tokens_grad = grad_inputs.astype(jnp.bfloat16)
    norm_local = jnp.stack([grad_gain_one, grad_gain_two])
    head_local = jnp.stack([grad_gain_query, grad_gain_key])
    owners = lax.axis_size("group")
    copies = lax.axis_size("dp")
    pieces = (
        lax.psum_scatter(
            joined_order(qkv_local, 0, owners, copies),
            ("dp", "group"),
            scatter_dimension=0,
            tiled=True,
        ),
        lax.psum_scatter(
            joined_order(out_local, 0, owners, copies),
            ("dp", "group"),
            scatter_dimension=0,
            tiled=True,
        ),
        lax.psum_scatter(
            joined_order(gate_up_local, 0, owners, copies),
            ("dp", "group"),
            scatter_dimension=0,
            tiled=True,
        ),
        lax.psum_scatter(
            joined_order(down_local, 0, owners, copies),
            ("dp", "group"),
            scatter_dimension=0,
            tiled=True,
        ),
        lax.psum_scatter(
            joined_order(norm_local, 1, owners, copies),
            ("dp", "group"),
            scatter_dimension=1,
            tiled=True,
        ),
        lax.psum_scatter(
            joined_order(head_local, 1, owners, copies),
            ("dp", "group"),
            scatter_dimension=1,
            tiled=True,
        ),
    )
    summed = (
        lax.all_gather(pieces[0], "dp", axis=0, tiled=True),
        lax.all_gather(pieces[1], "dp", axis=0, tiled=True),
        lax.all_gather(pieces[2], "dp", axis=0, tiled=True),
        lax.all_gather(pieces[3], "dp", axis=0, tiled=True),
        lax.all_gather(pieces[4], "dp", axis=1, tiled=True),
        lax.all_gather(pieces[5], "dp", axis=1, tiled=True),
    )
    squares = sum((jnp.sum(gradient * gradient) for gradient in summed))
    grad_total = lax.psum(squares, "group")
    clip_limit = math.sqrt(PARAMS)
    factor = clip_limit / jnp.maximum(jnp.sqrt(grad_total), clip_limit)
    masters = (qkv_weight, out_weight, gate_up_weight, down_weight, norm_gains, head_gains)
    moments = (qkv_moments, out_moments, gate_up_moments, down_moments, norm_moments, head_moments)
    rates = (LEARN_RATE, LEARN_RATE, LEARN_RATE, LEARN_RATE, GAIN_RATE, GAIN_RATE)
    decays = (WEIGHT_DECAY, WEIGHT_DECAY, WEIGHT_DECAY, WEIGHT_DECAY, 0.0, 0.0)
    renewed_all = []
    moments_all = []
    for master, moment, gradient, step_rate, decay_rate in zip(
        masters, moments, summed, rates, decays
    ):
        renewed, stacked = adam_update(master, moment, gradient, factor, step_rate, decay_rate)
        renewed_all.append(renewed)
        moments_all.append(stacked)
    column_index = lax.axis_index("dp")
    column_count = lax.axis_size("dp")
    return (
        output,
        tokens_grad,
        own_columns(summed[0], column_index, column_count),
        own_columns(summed[1], column_index, column_count),
        own_columns(summed[2], column_index, column_count),
        own_columns(summed[3], column_index, column_count),
        summed[4],
        summed[5],
        renewed_all[0],
        renewed_all[1],
        renewed_all[2],
        renewed_all[3],
        renewed_all[4],
        renewed_all[5],
        moments_all[0],
        moments_all[1],
        moments_all[2],
        moments_all[3],
        moments_all[4],
        moments_all[5],
    )


def solution(mesh):
    placed = (
        P(("dp", "group"), None),
        P(("dp", "group")),
        P(("dp", "group")),
        P(("dp", "group"), None),
        P("group", None),
        P("group", None),
        P("group", None),
        P("group", None),
        P(None, "group"),
        P(None, "group"),
        P(None, "group", None),
        P(None, "group", None),
        P(None, "group", None),
        P(None, "group", None),
        P(None, None, "group"),
        P(None, None, "group"),
    )
    return jax.shard_map(
        on_device,
        mesh=mesh,
        in_specs=placed,
        out_specs=(
            P(("dp", "group"), None),
            P(("dp", "group"), None),
            P("group", "dp"),
            P("group", "dp"),
            P("group", "dp"),
            P("group", "dp"),
            P(None, "group"),
            P(None, "group"),
            P("group", None),
            P("group", None),
            P("group", None),
            P("group", None),
            P(None, "group"),
            P(None, "group"),
            P(None, "group", None),
            P(None, "group", None),
            P(None, "group", None),
            P(None, "group", None),
            P(None, None, "group"),
            P(None, None, "group"),
        ),
        check_vma=False,
    )
```

profile of v0, /device:TPU:0, one launch (start us, length us, event | category | flops | bytes accessed | tf_op | source)
XLA Modules:
  0.0 1525.3 jit_solution(2794801300747954)
XLA Ops:
  35.1 37.2 %all-gather.12.cloned.1.call-done = bf16[1024,4096]{1,0:T(8,128)(2,1)} async-done(((bf16[256,4096]{1,0:T(8,128)(2,1)}), bf16[1024,4096]{1,0:T(8,128)(2,1)}) %all-gather.12.cloned.1.call-update) | async-done | bytes 8388624 | tf_op jit(solution)/shard_map/all_gather | solution.py:108
  72.4 7.4 fusion.63
  98.5 8.5 fusion.81
  107.0 8.2 exponential_reduce_fusion
  115.3 12.1 fusion.37
  133.9 59.3 %all-gather.16.cloned.1.call-done = bf16[1024,6144]{1,0:T(8,128)(2,1)} async-done(((bf16[256,6144]{1,0:T(8,128)(2,1)}), bf16[1024,6144]{1,0:T(8,128)(2,1)}) %all-gather.16.cloned.1.call-update) | async-done | bytes 12582928 | tf_op jit(solution)/shard_map/all_gather | solution.py:110
  193.2 14.6 fusion.79
  207.9 33.8 %all-gather.18.cloned.1.call-done = bf16[3072,1024]{1,0:T(8,128)(2,1)} async-done(((bf16[768,1024]{1,0:T(8,128)(2,1)}), bf16[3072,1024]{1,0:T(8,128)(2,1)}) %all-gather.18.cloned.1.call-update) | async-done | bytes 6291472 | tf_op jit(solution)/shard_map/all_gather | solution.py:111
  241.6 13.2 multiply_convert_fusion.1
  254.9 14.3 multiply_reduce_fusion.6
  279.2 10.4 fusion.82
  289.6 11.9 copy.233
  311.5 11.0 fusion
  322.6 12.8 fusion.5
  363.6 8.9 bitcast_convert_fusion
  387.4 7.8 fusion.11
  408.0 15.1 fusion.12
  423.0 17.7 %copy.232 = f32[8,4,32,6144]{3,2,1,0:T(8,128)} copy(f32[8,4,32,6144]{3,2,0,1:T(8,128)} %bitcast.333) | data formatting | bytes 50331648 | tf_op jit(solution)/shard_map/transpose | solution.py:69
  442.4 10.6 fusion.29
  455.0 130.7 %reduce-scatter.15.cloned.1.call-done = f32[96,1024]{1,0:T(8,128)} async-done(((f32[3072,1024]{1,0:T(8,128)}), f32[96,1024]{1,0:T(8,128)}) %reduce-scatter.15.cloned.1.call-update) | async-done | bytes 393232 | tf_op jit(solution)/shard_map/reduce_scatter | solution.py:260
  585.7 184.1 %reduce-scatter.9.cloned.1.call-done = f32[32,4096]{1,0:T(8,128)} async-done(((f32[1024,4096]{1,0:T(8,128)}), f32[32,4096]{1,0:T(8,128)}) %reduce-scatter.9.cloned.1.call-update) | async-done | bytes 524304 | tf_op jit(solution)/shard_map/reduce_scatter | solution.py:242
  769.9 251.2 %reduce-scatter.13.cloned.1.call-done = f32[32,6144]{1,0:T(8,128)} async-done(((f32[1024,6144]{1,0:T(8,128)}), f32[32,6144]{1,0:T(8,128)}) %reduce-scatter.13.cloned.1.call-update) | async-done | bytes 786448 | tf_op jit(solution)/shard_map/reduce_scatter | solution.py:254
  1021.5 40.2 %all-reduce = f32[2,128]{1,0:T(2,128)S(1)} all-reduce(f32[2,128]{1,0:T(2,128)S(1)} %reshape.437), channel_id=7, replica_groups=mesh['dp'=8,'group'=4] {'dp','group'}, use_global_device_ids=true, to_apply=%region_22.23.clone | all-reduce | flops 256 | bytes 2048
  1061.8 20.0 %all-gather.2 = f32[8,4,2]{1,2,0:T(2,128)S(1)} all-gather(f32[1,4,2]{1,2,0:T(2,128)S(1)} %dynamic-slice_bitcast_fusion), channel_id=1, replica_groups=mesh['dp'=8,'group'=4] {'dp'}, dimensions={0}, use_global_device_ids=true | all-gather | bytes 288 | tf_op jit(solution)/shard_map/all_gather | solution.py:285
  1093.1 66.1 %reduce-scatter.17.cloned.1.call-done = f32[32,2]{1,0:T(8,128)} async-done(((f32[1024,2]{1,0:T(8,128)}), f32[32,2]{1,0:T(8,128)}) %reduce-scatter.17.cloned.1.call-update) | async-done | bytes 272
  1160.0 16.3 %all-gather.1 = f32[8,32,2]{1,2,0:T(2,128)S(1)} all-gather(f32[1,32,2]{1,2,0:T(2,128)S(1)} %bitcast.382), channel_id=1, replica_groups=mesh['dp'=8,'group'=4] {'dp'}, dimensions={0}, use_global_device_ids=true | all-gather | bytes 2304 | tf_op jit(solution)/shard_map/all_gather | solution.py:284
  1177.0 29.3 %all-gather.22.cloned.1.call-done = f32[512,1024]{1,0:T(8,128)} async-done(((f32[64,1024]{1,0:T(8,128)}), f32[512,1024]{1,0:T(8,128)}) %all-gather.22.cloned.1.call-update) | async-done | bytes 2097168 | tf_op jit(solution)/shard_map/all_gather | solution.py:281
  1210.7 56.4 %all-gather.26.cloned.1.call-done = f32[768,1024]{1,0:T(8,128)} async-done(((f32[96,1024]{1,0:T(8,128)}), f32[768,1024]{1,0:T(8,128)}) %all-gather.26.cloned.1.call-update) | async-done | bytes 3145744 | tf_op jit(solution)/shard_map/all_gather | solution.py:283
  1272.2 68.4 %all-gather.20.cloned.1.call-done = f32[256,4096]{1,0:T(8,128)} async-done(((f32[32,4096]{1,0:T(8,128)}), f32[256,4096]{1,0:T(8,128)}) %all-gather.20.cloned.1.call-update) | async-done | bytes 4194320 | tf_op jit(solution)/shard_map/all_gather | solution.py:280
  1346.1 93.9 %all-gather.24.cloned.1.call-done = f32[256,6144]{1,0:T(8,128)} async-done(((f32[32,6144]{1,0:T(8,128)}), f32[256,6144]{1,0:T(8,128)}) %all-gather.24.cloned.1.call-update) | async-done | bytes 6291472 | tf_op jit(solution)/shard_map/all_gather | solution.py:282
  1470.3 13.3 fusion.45
  1483.6 10.9 pad_maximum_fusion
  (258 shorter events, 209.2 us)
Async XLA Ops:
  7.2 65.2 %all-gather.12.cloned.1.call-start = ((), (), s32[]{:S(2)}) async-start(), calls=%async_computation.5 | async-start | bytes 10485760 | tf_op jit(solution)/shard_map/all_gather | solution.py:108
  11.2 116.2 %all-gather.14.cloned.1.call-start = ((), (), s32[]{:S(2)}) async-start(), calls=%async_computation.6 | async-start | bytes 5242880 | tf_op jit(solution)/shard_map/all_gather | solution.py:109
  12.4 180.8 %all-gather.16.cloned.1.call-start = ((), (), s32[]{:S(2)}) async-start(), calls=%async_computation.7 | async-start | bytes 15728640 | tf_op jit(solution)/shard_map/all_gather | solution.py:110
  17.6 14.9 copy-start.51
  17.6 14.9 copy-start.45
  17.6 224.1 %all-gather.18.cloned.1.call-start = ((), (), s32[]{:S(2)}) async-start(), calls=%async_computation.8 | async-start | bytes 7864320 | tf_op jit(solution)/shard_map/all_gather | solution.py:111
  19.1 435.3 %reduce-scatter.11.cloned.1.call-start = ((), (), s32[]{:S(2)}) async-start(), calls=%async_computation.11 | async-start | bytes 8650752 | tf_op jit(solution)/shard_map/reduce_scatter | solution.py:248
  25.2 54.6 %copy-start.39 = (f32[1,1024]{1,0:T(1,128)}, f32[1,1024]{1,0:T(1,128)S(1)}, u32[]{:S(2)}) copy-start(f32[1,1024]{1,0:T(1,128)S(1)} %get-tuple-element.63) | copy-start | bytes 12292
  26.8 53.0 %copy-start.42 = (f32[512]{0:T(512)}, f32[512]{0:T(512)S(1)}, u32[]{:S(2)}) copy-start(f32[512]{0:T(512)S(1)} %add_rsqrt_fusion.3) | copy-start | bytes 6148
  35.1 56.0 %copy-start.33 = (f32[512,64]{1,0:T(8,128)}, f32[512,64]{1,0:T(8,128)S(1)}, u32[]{:S(2)}) copy-start(f32[512,64]{1,0:T(8,128)S(1)} %get-tuple-element.68) | copy-start | bytes 393220
  35.1 62.4 %copy-start.22 = (f32[512,64]{1,0:T(8,128)}, f32[512,64]{1,0:T(8,128)S(1)}, u32[]{:S(2)}) copy-start(f32[512,64]{1,0:T(8,128)S(1)} %get-tuple-element.69) | copy-start | bytes 393220
  80.1 16.8 %copy-start.5 = (f32[64,8,8,128]{3,2,1,0:T(8,128)}, f32[64,8,8,128]{3,2,1,0:T(8,128)S(1)}, u32[]{:S(2)}) copy-start(f32[64,8,8,128]{3,2,1,0:T(8,128)S(1)} %get-tuple-element.45) | copy-start | bytes 6291460
  207.9 47.0 %copy-start.14 = (f32[512,1024]{1,0:T(8,128)S(1)}, f32[512,1024]{1,0:T(8,128)}, u32[]{:S(2)}) copy-start(f32[512,1024]{1,0:T(8,128)} %get-tuple-element.75) | copy-start | bytes 6291460
  272.4 30.1 %copy-start.7 = (f32[512,1024]{1,0:T(8,128)}, f32[512,1024]{1,0:T(8,128)S(1)}, u32[]{:S(2)}) copy-start(f32[512,1024]{1,0:T(8,128)S(1)} %multiply_add_fusion.2) | copy-start | bytes 6291460
  279.0 306.7 %reduce-scatter.15.cloned.1.call-start = ((), (), s32[]{:S(2)}) async-start(), calls=%async_computation.15 | async-start | bytes 12976128 | tf_op jit(solution)/shard_map/reduce_scatter | solution.py:260
  301.6 468.3 %reduce-scatter.9.cloned.1.call-start = ((), (), s32[]{:S(2)}) async-start(), calls=%async_computation.9 | async-start | bytes 17301504 | tf_op jit(solution)/shard_map/reduce_scatter | solution.py:242
  322.5 12.9 copy-start.27
  373.1 22.2 %copy-start.30 = (bf16[512,1024]{1,0:T(8,128)(2,1)}, bf16[512,1024]{1,0:T(8,128)(2,1)S(1)}, u32[]{:S(2)}) copy-start(bf16[512,1024]{1,0:T(8,128)(2,1)S(1)} %copy.257) | copy-start | bytes 3145732
  406.4 614.7 %reduce-scatter.13.cloned.1.call-start = ((), (), s32[]{:S(2)}) async-start(), calls=%async_computation.13 | async-start | bytes 25952256 | tf_op jit(solution)/shard_map/reduce_scatter | solution.py:254
  440.8 718.5 %reduce-scatter.17.cloned.1.call-start = ((), (), s32[]{:S(2)}) async-start(), calls=%async_computation.17 | async-start | bytes 540672
  453.1 629.4 %copy-start.8 = (f32[512,1024]{1,0:T(8,128)S(1)}, f32[512,1024]{1,0:T(8,128)}, u32[]{:S(2)}) copy-start(f32[512,1024]{1,0:T(8,128)} %copy-done.7) | copy-start | bytes 6291460
  454.3 752.0 %all-gather.22.cloned.1.call-start = ((), (), s32[]{:S(2)}) async-start(), calls=%async_computation.12 | async-start | bytes 2359296 | tf_op jit(solution)/shard_map/all_gather | solution.py:281
  454.9 812.2 %all-gather.26.cloned.1.call-start = ((), (), s32[]{:S(2)}) async-start(), calls=%async_computation.16 | async-start | bytes 3538944 | tf_op jit(solution)/shard_map/all_gather | solution.py:283
  585.7 754.9 %all-gather.20.cloned.1.call-start = ((), (), s32[]{:S(2)}) async-start(), calls=%async_computation.10 | async-start | bytes 4718592 | tf_op jit(solution)/shard_map/all_gather | solution.py:280
  769.9 670.1 %all-gather.24.cloned.1.call-start = ((), (), s32[]{:S(2)}) async-start(), calls=%async_computation.14 | async-start | bytes 7077888 | tf_op jit(solution)/shard_map/all_gather | solution.py:282
  1081.9 374.7 %copy-start.49 = (f32[32,2]{0,1:T(2,128)}, f32[32,2]{0,1:T(2,128)S(1)}, u32[]{:S(2)}) copy-start(f32[32,2]{0,1:T(2,128)S(1)} %reshape.447) | copy-start | bytes 772
  1176.4 280.8 %copy-start.44 = (f32[256,2]{0,1:T(2,128)}, f32[256,2]{0,1:T(2,128)S(1)}, u32[]{:S(2)}) copy-start(f32[256,2]{0,1:T(2,128)S(1)} %reshape.445) | copy-start | bytes 6148
  1344.4 112.2 %copy-start.52 = (f32[2,2,32]{2,1,0:T(2,128)S(1)}, f32[2,2,32]{2,1,0:T(2,128)}, u32[]{:S(2)}) copy-start(f32[2,2,32]{2,1,0:T(2,128)} %param.31) | copy-start | bytes 1540
  1344.4 112.2 %copy-start.54 = (f32[2,32]{1,0:T(2,128)S(1)}, f32[2,32]{1,0:T(2,128)}, u32[]{:S(2)}) copy-start(f32[2,32]{1,0:T(2,128)} %param.25) | copy-start | bytes 772
  1344.4 112.8 %copy-start.47 = (f32[2,256]{1,0:T(2,128)S(1)}, f32[2,256]{1,0:T(2,128)}, u32[]{:S(2)}) copy-start(f32[2,256]{1,0:T(2,128)} %param.24) | copy-start | bytes 6148
  1344.4 112.8 %copy-start.50 = (f32[2,2,256]{2,1,0:T(2,128)S(1)}, f32[2,2,256]{2,1,0:T(2,128)}, u32[]{:S(2)}) copy-start(f32[2,2,256]{2,1,0:T(2,128)} %param.30) | copy-start | bytes 12292
  1344.4 114.6 %copy-start.10 = (f32[768,1024]{1,0:T(8,128)S(1)}, f32[768,1024]{1,0:T(8,128)}, u32[]{:S(2)}) copy-start(f32[768,1024]{1,0:T(8,128)} %all-gather.26.cloned.1.call-done) | copy-start | bytes 9437188
  (41 other events, 218.9 us)
Sparse Core Ops, SparseCore 0:
  11.3 60.9 all-gather.11
  74.5 34.4 all-gather.13
  111.1 82.0 all-gather.15
  195.2 46.3 all-gather.17
  279.1 149.9 reduce-scatter.10
  434.9 150.6 reduce-scatter.14
  588.0 181.8 reduce-scatter.8
  776.3 244.7 reduce-scatter.12
  1023.9 135.3 reduce-scatter.16
  1161.2 45.0 all-gather.21
  1208.5 58.5 all-gather.25
  1269.1 71.4 all-gather.19
  1342.7 97.2 all-gather.23
where the time goes:
time: 1540 us; the launch traced here: 1530 us
  waiting for transfers between devices  1010 us (66%)
  matrix products  162 us (11%)
  other arithmetic  145 us (9%)
  blocking collectives  94.4 us (6%)
  local copies, waits for them, and re-layouts  91.4 us (6%)
  between operations  20.3 us (1%)
    reduce_scatter x1, waiting for transfers between devices, on_device(): lax.psum_scatter(joined_order(gate_up_local, 0, owners, copies), ('dp', '...  251 us
    reduce_scatter x1, waiting for transfers between devices, on_device(): lax.psum_scatter(joined_order(qkv_local, 0, owners, copies), ('dp', 'grou...  184 us
    reduce_scatter x1, waiting for transfers between devices, on_device(): lax.psum_scatter(joined_order(down_local, 0, owners, copies), ('dp', 'gro...  131 us
    all_gather x1, waiting for transfers between devices, on_device(): lax.all_gather(pieces[2], 'dp', axis=0, tiled=True)  93.9 us
    all_gather x1, waiting for transfers between devices, on_device(): lax.all_gather(pieces[0], 'dp', axis=0, tiled=True)  68.4 us
    unnamed x14, waiting for transfers between devices  66.8 us
    all_gather x1, waiting for transfers between devices, on_device(): lax.all_gather(gate_up_weight.astype(jnp.bfloat16), 'group', axis=0, tile...  59.3 us
    another operation x12, other arithmetic, adam_update(): return (renewed, jnp.stack([first_moment, second]))  57.1 us
  transfers between devices with their start and end apart: 13, of which 11 were waited for; matrix products, arithmetic and copies ran while one was open for 18% of the time, Pallas kernels for 0%

commit v1 on v0

--- a/solution.py
+++ b/solution.py
@@ -20,6 +20,17 @@
 BETA_TWO = 0.95
 ADAM_EPS = 1e-08
 STEP_COUNT = 3.0
+
+
+def collect(x, axis, dim):
+    ways = lax.axis_size(axis)
+    pieces = [x]
+    for far in range(1, ways):
+        pieces.append(
+            lax.ppermute(pieces[far - 1], axis, [(d, (d - 1) % ways) for d in range(ways)])
+        )
+    line = jnp.concatenate(pieces, axis=dim)
+    return jnp.roll(line, lax.axis_index(axis) * x.shape[dim], axis=dim)
 
 
 def rotary_tables(places, width):
@@ -280,7 +291,7 @@
         lax.all_gather(pieces[0], "dp", axis=0, tiled=True),
         lax.all_gather(pieces[1], "dp", axis=0, tiled=True),
         lax.all_gather(pieces[2], "dp", axis=0, tiled=True),
-        lax.all_gather(pieces[3], "dp", axis=0, tiled=True),
+        collect(pieces[3], "dp", 0),
         lax.all_gather(pieces[4], "dp", axis=1, tiled=True),
         lax.all_gather(pieces[5], "dp", axis=1, tiled=True),
     )

time: 1540 us -> 1490 us (0.968)
  waiting for transfers between devices: 1010 us -> 929 us
  starting transfers between devices: 0.7 us -> 20.6 us
  local copies, waits for them, and re-layouts: 91.4 us -> 107 us
    all_gather x1 -> x0, waiting for transfers between devices: 56.4 us -> none  [on_device(): lax.all_gather(pieces[3], 'dp', axis=0, tiled=True)]
    unnamed x14 -> x13, waiting for transfers between devices: 66.8 us -> 33.8 us
    reduce_scatter x1, waiting for transfers between devices: 131 us -> 160 us  [on_device(): lax.psum_scatter(joined_order(down_local, 0, owners, copies), ('dp', 'gro...]
    reduce_scatter x1, waiting for transfers between devices: 184 us -> 156 us  [on_device(): lax.psum_scatter(joined_order(qkv_local, 0, owners, copies), ('dp', 'grou...]
    ppermute x0 -> x7, waiting for transfers between devices: none -> 26.5 us  [collect(): lax.ppermute(pieces[far - 1], axis, [(d, (d - 1) % ways) for d in range(w...]
    all_gather x1, waiting for transfers between devices: 29.3 us -> 2.92 us  [on_device(): lax.all_gather(pieces[1], 'dp', axis=0, tiled=True)]
    ppermute x0 -> x7, starting transfers between devices: none -> 20.1 us  [collect(): lax.ppermute(pieces[far - 1], axis, [(d, (d - 1) % ways) for d in range(w...]
    unnamed x135 -> x152, local copies, waits for them, and re-layouts: 33.1 us -> 45.7 us
  transfers between devices with their start and end apart: 13 -> 19, of which waited for: 11 -> 14; matrix products, arithmetic and copies ran while one was open for 18% -> 20% of each run, Pallas kernels for 0% -> 0%
where the time goes in v1:
time: 1490 us; the launch traced here: 1480 us
  waiting for transfers between devices  929 us (62%)
  matrix products  161 us (11%)
  other arithmetic  147 us (10%)
  local copies, waits for them, and re-layouts  107 us (7%)
  blocking collectives  93 us (6%)
  starting transfers between devices  20.6 us (1%)
  between operations  20.4 us (1%)
    reduce_scatter x1, waiting for transfers between devices, on_device(): lax.psum_scatter(joined_order(gate_up_local, 0, owners, copies), ('dp', '...  251 us
    reduce_scatter x1, waiting for transfers between devices, on_device(): lax.psum_scatter(joined_order(down_local, 0, owners, copies), ('dp', 'gro...  160 us
    reduce_scatter x1, waiting for transfers between devices, on_device(): lax.psum_scatter(joined_order(qkv_local, 0, owners, copies), ('dp', 'grou...  156 us
    all_gather x1, waiting for transfers between devices, on_device(): lax.all_gather(pieces[2], 'dp', axis=0, tiled=True)  93.7 us
    all_gather x1, waiting for transfers between devices, on_device(): lax.all_gather(pieces[0], 'dp', axis=0, tiled=True)  73.7 us
    all_gather x1, waiting for transfers between devices, on_device(): lax.all_gather(gate_up_weight.astype(jnp.bfloat16), 'group', axis=0, tile...  58.9 us
    another operation x12, other arithmetic, adam_update(): return (renewed, jnp.stack([first_moment, second]))  57.2 us
    unnamed x152, local copies, waits for them, and re-layouts  45.7 us
  transfers between devices with their start and end apart: 19, of which 14 were waited for; matrix products, arithmetic and copies ran while one was open for 20% of the time, Pallas kernels for 0%

profile of v1, /device:TPU:0, one launch (start us, length us, event | category | flops | bytes accessed | tf_op | source)
XLA Modules:
  0.0 1477.6 jit_solution(9795201867796685306)
XLA Ops:
  35.1 37.2 %all-gather.11.cloned.1.call-done = bf16[1024,4096]{1,0:T(8,128)(2,1)} async-done(((bf16[256,4096]{1,0:T(8,128)(2,1)}), bf16[1024,4096]{1,0:T(8,128)(2,1)}) %all-gather.11.cloned.1.call-update) | async-done | bytes 8388624 | tf_op jit(solution)/shard_map/all_gather | solution.py:119
  72.4 7.4 fusion.62
  98.5 8.7 fusion.81
  107.2 8.3 exponential_reduce_fusion
  115.6 12.2 fusion.37
  134.3 58.9 %all-gather.15.cloned.1.call-done = bf16[1024,6144]{1,0:T(8,128)(2,1)} async-done(((bf16[256,6144]{1,0:T(8,128)(2,1)}), bf16[1024,6144]{1,0:T(8,128)(2,1)}) %all-gather.15.cloned.1.call-update) | async-done | bytes 12582928 | tf_op jit(solution)/shard_map/all_gather | solution.py:121
  193.2 14.6 fusion.79
  207.9 33.8 %all-gather.17.cloned.1.call-done = bf16[3072,1024]{1,0:T(8,128)(2,1)} async-done(((bf16[768,1024]{1,0:T(8,128)(2,1)}), bf16[3072,1024]{1,0:T(8,128)(2,1)}) %all-gather.17.cloned.1.call-update) | async-done | bytes 6291472 | tf_op jit(solution)/shard_map/all_gather | solution.py:122
  241.6 13.0 multiply_convert_fusion.1
  254.7 14.3 multiply_reduce_fusion.6
  288.6 10.8 fusion
  299.4 12.9 fusion.5
  340.8 8.7 bitcast_convert_fusion
  364.7 7.5 fusion.11
  384.9 14.9 %fusion.12 = f32[1024,6144]{1,0:T(8,128)} fusion(bf16[512,3072]{1,0:T(8,128)(2,1)} %get-tuple-element.30, bf16[512,3072]{1,0:T(8,128)(2,1)} %get-tuple-element.29, f32[512,1024]{1,0:T(8,128)S(1)} %copy-done.15, f32[1024]{0:T(1024)S(1)} %bitcast.375, f32[512]{0:T(512)S(1)} %add_rsqrt_fusion.2), kind=kOutput, calls=%fused_computation.47 | convolution fusion | flops 6456606720 | bytes 33560576 | tf_op jit(solution)/shard_map/dot_general | solution.py:59
  399.9 17.6 %copy.232 = f32[8,4,32,6144]{3,2,1,0:T(8,128)} copy(f32[8,4,32,6144]{3,2,0,1:T(8,128)} %bitcast.333) | data formatting | bytes 50331648 | tf_op jit(solution)/shard_map/transpose | solution.py:80
  418.7 8.6 fusion.82
  427.2 12.0 copy.233
  440.9 10.9 fusion.29
  453.6 156.4 %reduce-scatter.9.cloned.1.call-done = f32[32,4096]{1,0:T(8,128)} async-done(((f32[1024,4096]{1,0:T(8,128)}), f32[32,4096]{1,0:T(8,128)}) %reduce-scatter.9.cloned.1.call-update) | async-done | bytes 524304 | tf_op jit(solution)/shard_map/reduce_scatter | solution.py:253
  610.1 251.2 %reduce-scatter.13.cloned.1.call-done = f32[32,6144]{1,0:T(8,128)} async-done(((f32[1024,6144]{1,0:T(8,128)}), f32[32,6144]{1,0:T(8,128)}) %reduce-scatter.13.cloned.1.call-update) | async-done | bytes 786448 | tf_op jit(solution)/shard_map/reduce_scatter | solution.py:265
  861.3 160.3 %reduce-scatter.15.cloned.1.call-done = f32[96,1024]{1,0:T(8,128)} async-done(((f32[3072,1024]{1,0:T(8,128)}), f32[96,1024]{1,0:T(8,128)}) %reduce-scatter.15.cloned.1.call-update) | async-done | bytes 393232 | tf_op jit(solution)/shard_map/reduce_scatter | solution.py:271
  1048.1 8.7 add_convert_fusion.1
  1062.4 38.6 %all-reduce = f32[2,128]{1,0:T(2,128)S(1)} all-reduce(f32[2,128]{1,0:T(2,128)S(1)} %reshape.437), channel_id=7, replica_groups=mesh['dp'=8,'group'=4] {'dp','group'}, use_global_device_ids=true, to_apply=%region_22.23.clone | all-reduce | flops 256 | bytes 2048
  1101.1 20.3 %all-gather.2 = f32[8,4,2]{1,2,0:T(2,128)S(1)} all-gather(f32[1,4,2]{1,2,0:T(2,128)S(1)} %dynamic-slice_bitcast_fusion), channel_id=1, replica_groups=mesh['dp'=8,'group'=4] {'dp'}, dimensions={0}, use_global_device_ids=true | all-gather | bytes 288 | tf_op jit(solution)/shard_map/all_gather | solution.py:296
  1127.1 33.1 %reduce-scatter.17.cloned.1.call-done = f32[32,2]{1,0:T(8,128)} async-done(((f32[1024,2]{1,0:T(8,128)}), f32[32,2]{1,0:T(8,128)}) %reduce-scatter.17.cloned.1.call-update) | async-done | bytes 272
  1161.0 16.3 %all-gather.1 = f32[8,32,2]{1,2,0:T(2,128)S(1)} all-gather(f32[1,32,2]{1,2,0:T(2,128)S(1)} %bitcast.382), channel_id=1, replica_groups=mesh['dp'=8,'group'=4] {'dp'}, dimensions={0}, use_global_device_ids=true | all-gather | bytes 2304 | tf_op jit(solution)/shard_map/all_gather | solution.py:295
  1193.5 9.9 collective-permute-done.6
  1219.2 73.7 %all-gather.19.cloned.1.call-done = f32[256,4096]{1,0:T(8,128)} async-done(((f32[32,4096]{1,0:T(8,128)}), f32[256,4096]{1,0:T(8,128)}) %all-gather.19.cloned.1.call-update) | async-done | bytes 4194320 | tf_op jit(solution)/shard_map/all_gather | solution.py:291
  1298.5 93.7 %all-gather.23.cloned.1.call-done = f32[256,6144]{1,0:T(8,128)} async-done(((f32[32,6144]{1,0:T(8,128)}), f32[256,6144]{1,0:T(8,128)}) %all-gather.23.cloned.1.call-update) | async-done | bytes 6291472 | tf_op jit(solution)/shard_map/all_gather | solution.py:293
  1422.6 13.3 fusion.45
  1435.8 10.9 pad_maximum_fusion
  (287 shorter events, 258.6 us)
Async XLA Ops:
  7.2 65.2 %all-gather.11.cloned.1.call-start = ((), (), s32[]{:S(2)}) async-start(), calls=%async_computation.5 | async-start | bytes 10485760 | tf_op jit(solution)/shard_map/all_gather | solution.py:119
  11.2 116.6 %all-gather.13.cloned.1.call-start = ((), (), s32[]{:S(2)}) async-start(), calls=%async_computation.6 | async-start | bytes 5242880 | tf_op jit(solution)/shard_map/all_gather | solution.py:120
  12.4 180.8 %all-gather.15.cloned.1.call-start = ((), (), s32[]{:S(2)}) async-start(), calls=%async_computation.7 | async-start | bytes 15728640 | tf_op jit(solution)/shard_map/all_gather | solution.py:121
  17.6 224.1 %all-gather.17.cloned.1.call-start = ((), (), s32[]{:S(2)}) async-start(), calls=%async_computation.8 | async-start | bytes 7864320 | tf_op jit(solution)/shard_map/all_gather | solution.py:122
  19.1 434.0 %reduce-scatter.11.cloned.1.call-start = ((), (), s32[]{:S(2)}) async-start(), calls=%async_computation.11 | async-start | bytes 8650752 | tf_op jit(solution)/shard_map/reduce_scatter | solution.py:259
  25.2 54.6 %copy-start.41 = (f32[1,1024]{1,0:T(1,128)}, f32[1,1024]{1,0:T(1,128)S(1)}, u32[]{:S(2)}) copy-start(f32[1,1024]{1,0:T(1,128)S(1)} %get-tuple-element.63) | copy-start | bytes 12292
  26.8 52.9 %copy-start.44 = (f32[512]{0:T(512)}, f32[512]{0:T(512)S(1)}, u32[]{:S(2)}) copy-start(f32[512]{0:T(512)S(1)} %add_rsqrt_fusion.3) | copy-start | bytes 6148
  35.1 56.0 %copy-start.31 = (f32[512,64]{1,0:T(8,128)}, f32[512,64]{1,0:T(8,128)S(1)}, u32[]{:S(2)}) copy-start(f32[512,64]{1,0:T(8,128)S(1)} %get-tuple-element.68) | copy-start | bytes 393220
  278.8 331.2 %reduce-scatter.9.cloned.1.call-start = ((), (), s32[]{:S(2)}) async-start(), calls=%async_computation.9 | async-start | bytes 17301504 | tf_op jit(solution)/shard_map/reduce_scatter | solution.py:253
  383.4 477.9 %reduce-scatter.13.cloned.1.call-start = ((), (), s32[]{:S(2)}) async-start(), calls=%async_computation.13 | async-start | bytes 25952256 | tf_op jit(solution)/shard_map/reduce_scatter | solution.py:265
  417.5 604.1 %reduce-scatter.15.cloned.1.call-start = ((), (), s32[]{:S(2)}) async-start(), calls=%async_computation.15 | async-start | bytes 12976128 | tf_op jit(solution)/shard_map/reduce_scatter | solution.py:271
  439.3 720.9 %reduce-scatter.17.cloned.1.call-start = ((), (), s32[]{:S(2)}) async-start(), calls=%async_computation.16 | async-start | bytes 540672
  453.0 761.8 %all-gather.21.cloned.1.call-start = ((), (), s32[]{:S(2)}) async-start(), calls=%async_computation.12 | async-start | bytes 2359296 | tf_op jit(solution)/shard_map/all_gather | solution.py:292
  453.6 839.4 %all-gather.19.cloned.1.call-start = ((), (), s32[]{:S(2)}) async-start(), calls=%async_computation.10 | async-start | bytes 4718592 | tf_op jit(solution)/shard_map/all_gather | solution.py:291
  610.0 782.2 %all-gather.23.cloned.1.call-start = ((), (), s32[]{:S(2)}) async-start(), calls=%async_computation.14 | async-start | bytes 7077888 | tf_op jit(solution)/shard_map/all_gather | solution.py:293
  1021.6 9.8 collective-permute-start
  1031.4 10.8 collective-permute-start.1
  1036.6 87.4 %copy-start.8 = (f32[512,1024]{1,0:T(8,128)S(1)}, f32[512,1024]{1,0:T(8,128)}, u32[]{:S(2)}) copy-start(f32[512,1024]{1,0:T(8,128)} %copy-done.7) | copy-start | bytes 6291460
  1042.2 17.8 %collective-permute-start.2 = (f32[96,1024]{1,0:T(8,128)}, f32[96,1024]{1,0:T(8,128)}, u32[]{:S(2)}, u32[]{:S(2)}) collective-permute-start(f32[96,1024]{1,0:T(8,128)} %collective-permute-done.1), channel_id=1, source_target_pairs={{0,28},{4,0},{8,4},{12,8},{16,12},{20,16},{24,20},{28,24},{1,29},{... | collective-permute-start | bytes 1179656 | tf_op jit(solution)/shard_map/ppermute | solution.py:30
  1056.8 123.5 %copy-start.35 = (f32[96,1024]{1,0:T(8,128)S(1)}, f32[96,1024]{1,0:T(8,128)}, u32[]{:S(2)}) copy-start(f32[96,1024]{1,0:T(8,128)} %reduce-scatter.15.cloned.1.call-done) | copy-start | bytes 1179652
  1060.1 62.6 %collective-permute-start.3 = (f32[96,1024]{1,0:T(8,128)}, f32[96,1024]{1,0:T(8,128)}, u32[]{:S(2)}, u32[]{:S(2)}) collective-permute-start(f32[96,1024]{1,0:T(8,128)} %collective-permute-done.2), channel_id=1, source_target_pairs={{0,28},{4,0},{8,4},{12,8},{16,12},{20,16},{24,20},{28,24},{1,29},{... | collective-permute-start | bytes 1179656 | tf_op jit(solution)/shard_map/ppermute | solution.py:30
  1122.7 54.7 %collective-permute-start.4 = (f32[96,1024]{1,0:T(8,128)}, f32[96,1024]{1,0:T(8,128)}, u32[]{:S(2)}, u32[]{:S(2)}) collective-permute-start(f32[96,1024]{1,0:T(8,128)} %collective-permute-done.3), channel_id=1, source_target_pairs={{0,28},{4,0},{8,4},{12,8},{16,12},{20,16},{24,20},{28,24},{1,29},{... | collective-permute-start | bytes 1179656 | tf_op jit(solution)/shard_map/ppermute | solution.py:30
  1127.1 76.3 %copy-start.37 = (f32[96,1024]{1,0:T(8,128)S(1)}, f32[96,1024]{1,0:T(8,128)}, u32[]{:S(2)}) copy-start(f32[96,1024]{1,0:T(8,128)} %copy-done.36) | copy-start | bytes 1179652
  1177.4 232.0 %copy-start.46 = (f32[256,2]{0,1:T(2,128)}, f32[256,2]{0,1:T(2,128)S(1)}, u32[]{:S(2)}) copy-start(f32[256,2]{0,1:T(2,128)S(1)} %reshape.445) | copy-start | bytes 6148
  1177.4 8.9 collective-permute-start.5
  1186.3 17.0 %collective-permute-start.6 = (f32[96,1024]{1,0:T(8,128)S(1)}, f32[96,1024]{1,0:T(8,128)S(1)}, u32[]{:S(2)}, u32[]{:S(2)}) collective-permute-start(f32[96,1024]{1,0:T(8,128)S(1)} %collective-permute-done.5), channel_id=1, source_target_pairs={{0,28},{4,0},{8,4},{12,8},{16,12},{20,16},{24,20},{28,24},{1,29},{... | collective-permute-start | bytes 1179656 | tf_op jit(solution)/shard_map/ppermute | solution.py:30
  1296.8 112.0 %copy-start.51 = (f32[32,2]{0,1:T(2,128)S(1)}, f32[32,2]{0,1:T(2,128)}, u32[]{:S(2)}) copy-start(f32[32,2]{0,1:T(2,128)} %reshape.447) | copy-start | bytes 772
  1296.8 112.0 %copy-start.54 = (f32[2,2,32]{2,1,0:T(2,128)S(1)}, f32[2,2,32]{2,1,0:T(2,128)}, u32[]{:S(2)}) copy-start(f32[2,2,32]{2,1,0:T(2,128)} %param.31) | copy-start | bytes 1540
  1296.8 112.0 %copy-start.56 = (f32[2,32]{1,0:T(2,128)S(1)}, f32[2,32]{1,0:T(2,128)}, u32[]{:S(2)}) copy-start(f32[2,32]{1,0:T(2,128)} %param.25) | copy-start | bytes 772
  1296.8 112.6 %copy-start.49 = (f32[2,256]{1,0:T(2,128)S(1)}, f32[2,256]{1,0:T(2,128)}, u32[]{:S(2)}) copy-start(f32[2,256]{1,0:T(2,128)} %param.24) | copy-start | bytes 6148
  1296.8 112.6 %copy-start.52 = (f32[2,2,256]{2,1,0:T(2,128)S(1)}, f32[2,2,256]{2,1,0:T(2,128)}, u32[]{:S(2)}) copy-start(f32[2,2,256]{2,1,0:T(2,128)} %param.30) | copy-start | bytes 12292
  1296.8 113.2 %copy-start.11 = (f32[768,1024]{1,0:T(8,128)S(1)}, f32[768,1024]{1,0:T(8,128)}, u32[]{:S(2)}) copy-start(f32[768,1024]{1,0:T(8,128)} %param.23) | copy-start | bytes 9437188
  (48 other events, 359.4 us)
Sparse Core Ops, SparseCore 0:
  11.3 60.9 all-gather.10
  74.5 34.4 all-gather.12
  111.1 82.0 all-gather.14
  195.2 46.3 all-gather.16
  278.9 150.1 reduce-scatter.10
  431.2 178.7 reduce-scatter.8
  616.4 244.7 reduce-scatter.12
  867.3 154.2 reduce-scatter.14
  1024.4 135.7 reduce-scatter.16
  1162.2 52.5 all-gather.20
  1216.9 75.9 all-gather.18
  1295.0 97.2 all-gather.22
